TPU v7x, 128 devices: a whole 4x4x4 slice. The times are simulated.
128 devices in a mesh: row: 8 (over z, core), col: 16 (over x, y).
Axes of the slice: x: 4, y: 4, z: 4, core: 2. Of those that a mesh axis runs over, the one named last changes fastest.
Arguments:
- trial_factor: bfloat16 [2, 8192, 512], P(None, ('row', 'col')), may hold values from -6 to 6
- occupied: bfloat16 [8192, 512], P(('col', 'row')), may hold values from -0.25 to 0.25
- centers: float32 [3, 8192], P(None, ('row', 'col')), may hold values from 0 to 1
- exponents: float32 [8192], P(('row', 'col')), may hold values from 0.5 to 4
- wave_vectors: float32 [3, 8192], P(None, ('row', 'col')), may hold values from -36 to 36
- phases: float32 [8192], P(('row', 'col')), may hold values from -3.140625 to 3.140625
- points: float32 [256, 3, 1024], P(('row', 'col')), may hold values from 0 to 1
- density: float32 [256, 1024], P(('row', 'col')), may hold values from 0.05 to 1
- weights: float32 [256, 1024], P(('row', 'col')), may hold values from 0.0001 to 0.001
- sources: int32 [256, 8, 1], P(('row', 'col')), may hold values from 0 to 15; in each aligned block of 16 rows (0 to 15, 16 to 31, ..., all dimensions but the last counted through in order) at most 2 rows name the same one
Outputs:
- response: float32 [8192, 2, 512], P(('row', 'col'))
Inputs may be any that keep to these rules, and one draw needn't show every extreme that they name: `sources`: among the 16 entries of the batches of one device, no column block is named more than 2 times, and some block exactly 2 times.
All inputs are finite; a program needn't handle non-finite values.
Results may differ from a plain program's by a relative error of at most 0.0065.
Values may be sent and summed in bfloat16 or wider, within the bound.
A program may use at most 128 MiB of HBM per device.

v0:
```python
import jax
import jax.numpy as jnp
from jax import lax
from jax.sharding import PartitionSpec as P

TB = 256


EXCHANGE_COEF = 0.75 * (3.0 / 3.141592653589793) ** (1.0 / 3.0)


def rows_first(arrays, axis, dims):
    turned = [jnp.moveaxis(a, dim, 0) for a, dim in zip(arrays, dims)]
    both = jnp.concatenate([t.reshape(len(t), -1) for t in turned], axis=1)
    filled, at, finished = (lax.all_gather(both, axis, axis=0, tiled=True), 0, [])
    for t, dim in zip(turned, dims):
        slab = filled[:, at : at + t[0].size].reshape(-1, *t.shape[1:])
        finished.append(jnp.moveaxis(slab, 0, dim))
        at += t[0].size
    return tuple(finished)


def joined_along(tiles, dim):
    tiles = jnp.moveaxis(tiles, 0, dim)
    shape = tiles.shape
    return tiles.reshape(*shape[:dim], shape[dim] * shape[dim + 1], *shape[dim + 2 :])


def sent_to_all(value, axis):
    size = lax.axis_size(axis)
    return lax.all_to_all(
        jnp.broadcast_to(value[None], (size, *value.shape)), axis, 0, 0, tiled=True
    )


def gather_directly(value, axis, dim):
    return joined_along(sent_to_all(value, axis), dim)


def split_up(value, dim, size):
    shape = value.shape
    tiles = value.reshape(*shape[:dim], size, shape[dim] // size, *shape[dim + 1 :])
    return jnp.moveaxis(tiles, dim, 0)


def sum_at_owner(value, axis, dim):
    size = lax.axis_size(axis)
    tiles = lax.all_to_all(split_up(value, dim, size), axis, 0, 0, tiled=True)
    return jnp.sum(tiles.astype(jnp.float32), axis=0)


def collocate(grid_points, func_centers, func_exponents, func_waves, func_phases):
    npoints = grid_points.shape[1]
    nfuncs = func_centers.shape[1]
    radius = jnp.zeros((npoints, nfuncs), jnp.float32)
    phase_sum = jnp.zeros((npoints, nfuncs), jnp.float32) + func_phases[None, :]
    for coordinate in range(3):
        offset = grid_points[coordinate][:, None] - func_centers[coordinate][None, :]
        radius = radius + offset * offset
        phase_sum = phase_sum + grid_points[coordinate][:, None] * func_waves[coordinate][None, :]
    return (jnp.exp(-func_exponents[None, :] * radius) * jnp.cos(phase_sum)).astype(jnp.bfloat16)


def batch_response(ground, quad_weights, row_values, col_values, pair_tiles):
    npoints = col_values.shape[0]
    row_tiles = pair_tiles.shape[0]
    col_span = pair_tiles.shape[1]
    tile_width = pair_tiles.shape[2]
    tile_size = row_values.shape[1] // row_tiles
    vectors = tile_width // tile_size
    col_phi = col_values.reshape(npoints, row_tiles, col_span)
    half_contracted = jnp.einsum(
        "gax,axy->gay", col_phi, pair_tiles, preferred_element_type=jnp.float32
    )
    half_contracted = half_contracted.reshape(npoints, row_tiles, vectors, tile_size)
    row_phi = row_values.astype(jnp.float32).reshape(npoints, row_tiles, 1, tile_size)
    response_density = jnp.sum(half_contracted * row_phi, axis=(1, 3))
    kernel = -(4.0 / 9.0) * EXCHANGE_COEF * jnp.exp(-(2.0 / 3.0) * jnp.log(ground))
    potential = (quad_weights * kernel)[:, None] * response_density
    scaled = (
        (potential[:, None, :, None] * row_phi)
        .astype(jnp.bfloat16)
        .reshape(npoints, row_tiles, tile_width)
    )
    matrix = jnp.einsum("gax,gay->axy", col_phi, scaled, preferred_element_type=jnp.float32)
    return matrix.astype(jnp.bfloat16)


def per_device(
    trial_factor,
    occupied,
    centers,
    exponents,
    wave_vectors,
    phases,
    points,
    density,
    weights,
    sources,
):
    columns = lax.axis_size("col")
    row_block = lax.axis_index("row")
    all_centers, all_waves, all_exponents, all_phases = rows_first(
        (centers, wave_vectors, exponents, phases), ("row", "col"), (1, 1, 0, 0)
    )
    col_factor = gather_directly(occupied, "row", 0)
    span_col = col_factor.shape[0]
    orbital_count = col_factor.shape[1]
    tiles_col = span_col // TB
    span_row = trial_factor.shape[1] * columns
    tiles_row = span_row // TB
    vectors = trial_factor.shape[0]
    pair_count = tiles_row * tiles_col
    batch_count = sources.shape[0]
    slot_count = batch_count * pair_count
    slot_source = sources.reshape(slot_count)
    capacity = max(2, (slot_count + columns - 1) // columns)
    source_hot = (slot_source[:, None] == jnp.arange(columns, dtype=jnp.int32)[None, :]).astype(
        jnp.int32
    )
    slot_rank = jnp.sum(source_hot * (jnp.cumsum(source_hot, axis=0) - 1), axis=1)
    slot_place = slot_source * capacity + slot_rank
    slot_pair = jnp.arange(slot_count, dtype=jnp.int32) % pair_count
    place_hot = slot_place[:, None] == jnp.arange(columns * capacity, dtype=jnp.int32)[None, :]
    place_matrix = place_hot.astype(jnp.bfloat16)
    wanted = jnp.sum(place_hot.astype(jnp.int32) * (slot_pair[:, None] + 1), axis=0) - 1
    asked_pairs = lax.all_to_all(
        wanted.reshape(columns, capacity), "col", split_axis=0, concat_axis=0, tiled=True
    )
    asked_flat = asked_pairs.reshape(columns * capacity)
    asked_col = jnp.where(asked_flat >= 0, asked_flat % tiles_col, -1)
    col_hot = (asked_col[:, None] == jnp.arange(tiles_col, dtype=jnp.int32)[None, :]).astype(
        jnp.bfloat16
    )
    row_start = row_block * span_row
    row_centers = lax.dynamic_slice_in_dim(all_centers, row_start, span_row, 1)
    row_waves = lax.dynamic_slice_in_dim(all_waves, row_start, span_row, 1)
    row_exponents = lax.dynamic_slice_in_dim(all_exponents, row_start, span_row, 0)
    row_phases = lax.dynamic_slice_in_dim(all_phases, row_start, span_row, 0)
    tile_offsets = jnp.arange(TB, dtype=jnp.int32)
    column_tile = slot_source * tiles_col + slot_pair % tiles_col
    column_index = (column_tile[:, None] * TB + tile_offsets[None, :]).reshape(
        batch_count, pair_count * TB
    )
    row_trial = gather_directly(trial_factor, "col", 1)
    row_split = row_trial.reshape(vectors, tiles_row, TB, orbital_count)
    outgoing_rows = (
        jnp.dot(
            col_hot,
            col_factor.reshape(tiles_col, TB * orbital_count),
            preferred_element_type=jnp.float32,
        )
        .astype(jnp.bfloat16)
        .reshape(columns, capacity, TB * orbital_count)
    )
    incoming_rows = lax.all_to_all(outgoing_rows, "col", split_axis=0, concat_axis=0, tiled=True)
    slot_rows = jnp.dot(
        place_matrix,
        incoming_rows.reshape(columns * capacity, TB * orbital_count),
        preferred_element_type=jnp.float32,
    ).astype(jnp.bfloat16)
    slot_rows = slot_rows.reshape(batch_count, tiles_row, tiles_col * TB, orbital_count)
    accumulated = jnp.zeros((span_row, vectors, orbital_count), jnp.float32)
    for position in range(batch_count):
        factor_rows = slot_rows[position]
        tiles_now = (
            jnp.einsum("kami,axi->axkm", row_split, factor_rows, preferred_element_type=jnp.float32)
            .astype(jnp.bfloat16)
            .reshape(tiles_row, tiles_col * TB, vectors * TB)
        )
        index_now = column_index[position]
        row_values = collocate(points[position], row_centers, row_exponents, row_waves, row_phases)
        col_values = collocate(
            points[position],
            jnp.take(all_centers, index_now, axis=1),
            jnp.take(all_exponents, index_now),
            jnp.take(all_waves, index_now, axis=1),
            jnp.take(all_phases, index_now),
        )
        potential_now = batch_response(
            density[position], weights[position], row_values, col_values, tiles_now
        )
        contrib = jnp.einsum(
            "axkm,axi->amki",
            potential_now.reshape(tiles_row, tiles_col * TB, vectors, TB),
            factor_rows,
            preferred_element_type=jnp.float32,
        )
        accumulated = accumulated + contrib.reshape(span_row, vectors, orbital_count)
    return sum_at_owner(accumulated.astype(jnp.bfloat16), "col", 0)


def solution(mesh):
    in_specs = (
        P(None, ("row", "col"), None),
        P(("col", "row"), None),
        P(None, ("row", "col")),
        P(("row", "col")),
        P(None, ("row", "col")),
        P(("row", "col")),
        P(("row", "col"), None, None),
        P(("row", "col"), None),
        P(("row", "col"), None),
        P(("row", "col"), None, None),
    )
    out_specs = P(("row", "col"), None, None)
    return jax.shard_map(
        per_device, mesh=mesh, in_specs=in_specs, out_specs=out_specs, check_vma=False
    )
```

profile of v0, /device:TPU:1, one launch (start us, length us, event | category | flops | bytes accessed | tf_op | source)
XLA Modules:
  0.0 500.0 jit_solution(6194793369204841043)
XLA Ops:
  0.0 0.5 broadcast.560
  0.5 1.3 reduce.54
  2.1 0.2 select_reduce_fusion.1
  2.3 0.1 select_reduce_fusion
  2.4 13.8 %all_to_all.26 = s32[16,1,2]{2,1,0:T(1,128)S(1)} all-to-all(s32[16,1,2]{2,1,0:T(1,128)S(1)} %bitcast.131), channel_id=1, replica_groups=mesh['row'=8,'col'=16] {'col'}, dimensions={0} | all-to-all | bytes 256 | tf_op jit(solution)/shard_map/all_to_all | solution.py:127
  16.3 0.9 broadcast_in_dim.16
  17.1 16.5 %all_to_all.27 = bf16[8,64,512]{2,1,0:T(8,128)(2,1)S(1)} all-to-all(bf16[8,64,512]{2,1,0:T(8,128)(2,1)S(1)} %broadcast_in_dim.16), channel_id=1, replica_groups=mesh['row'=8,'col'=16] {'row'}, dimensions={0} | all-to-all | bytes 1048576 | tf_op jit(solution)/shard_map/all_to_all | solution.py:31
  33.7 2.5 broadcast_in_dim.17
  36.1 3.7 all-to-all-start.3
  40.0 73.7 %all-gather = f32[128,64,8]{1,2,0:T(8,128)S(1)} all-gather(f32[1,64,8]{1,2,0:T(8,128)S(1)} %maximum_bitcast_fusion), channel_id=1, replica_groups=mesh['row'=8,'col'=16] {'row','col'}, dimensions={0}, use_global_device_ids=true | all-gather | bytes 264192 | tf_op jit(solution)/shard_map/all_gather | solution.py:15
  113.7 2.6 copy.26
  116.3 0.7 reduce.55
  117.1 0.4 reshape_reshape.6
  117.5 5.6 %convolution_convert_fusion = bf16[32,131072]{1,0:T(8,128)(2,1)} fusion(bf16[2,131072]{1,0:T(2,128)(2,1)S(1)} %reshape_reshape.6, s32[32]{0:T(128)S(1)} %compare_select_fusion.6), kind=kOutput, calls=%fused_computation.8 | convolution fusion | flops 20971584 | bytes 8913024 | tf_op jit(solution)/shard_map/dot_general | solution.py:148
  123.1 9.4 %reshape.626 = bf16[16,2,131072]{2,1,0:T(2,128)(2,1)} reshape(bf16[32,131072]{1,0:T(8,128)(2,1)} %convolution_convert_fusion) | data formatting | bytes 16777216 | tf_op jit(solution)/shard_map/reshape | solution.py:154
  132.4 1.4 copy-done.3
  133.8 5.3 %all-to-all-start.2 = ((bf16[16,2,131072]{2,1,0:T(2,128)(2,1)}), bf16[16,2,131072]{2,1,0:T(2,128)(2,1)}, u32[]{:S(2)}, u32[]{:S(2)}) async-start(bf16[16,2,131072]{2,1,0:T(2,128)(2,1)} %reshape.626), calls=%async_computation.2 | async-start | bytes 16777216 | tf_op jit(solution)/shard_map/all_to_all | solution.py:156
  139.1 9.0 %slice_reduce_fusion.19 = (f32[8192]{0:T(1024)S(1)}, f32[8192]{0:T(1024)S(1)}, f32[8192,1]{1,0:T(8,128)}, f32[8192,1]{1,0:T(8,128)}) fusion(f32[8192,8]{1,0:T(8,128)} %bitcast.98), kind=kLoop, calls=%fused_computation.112 | loop fusion | bytes 196608 | tf_op jit(solution)/shard_map/slice | solution.py:17
  148.0 11.8 %gather_fusion.4 = f32[2048]{0:T(1024)S(1)} fusion(f32[8192]{0:T(1024)S(1)} %get-tuple-element.6, s32[2048]{0:T(1024)S(1)} %fusion.27), kind=kCustom, calls=%fused_computation.3.clone | custom fusion | bytes 24576 | tf_op jit(solution)/shard_map/jit(_take)/gather | solution.py:176
  159.8 11.8 %gather_fusion = f32[2048]{0:T(1024)S(1)} fusion(f32[8192]{0:T(1024)S(1)} %get-tuple-element.6, s32[2048]{0:T(1024)S(1)} %fusion.26), kind=kCustom, calls=%fused_computation.clone | custom fusion | bytes 24576 | tf_op jit(solution)/shard_map/jit(_take)/gather | solution.py:176
  171.6 11.8 %gather_fusion.6 = f32[2048]{0:T(1024)S(1)} fusion(f32[8192]{0:T(1024)S(1)} %get-tuple-element.8, s32[2048]{0:T(1024)S(1)} %fusion.27), kind=kCustom, calls=%fused_computation.4.clone | custom fusion | bytes 24576 | tf_op jit(solution)/shard_map/jit(_take)/gather | solution.py:178
  183.4 11.8 %gather_fusion.2 = f32[2048]{0:T(1024)S(1)} fusion(f32[8192]{0:T(1024)S(1)} %get-tuple-element.8, s32[2048]{0:T(1024)S(1)} %fusion.26), kind=kCustom, calls=%fused_computation.2.clone | custom fusion | bytes 24576 | tf_op jit(solution)/shard_map/jit(_take)/gather | solution.py:178
  195.2 10.6 %slice_bitcast_fusion.3 = (f32[3,8192]{0,1:T(8,128)}, f32[3,8192]{0,1:T(8,128)}, f32[8192,3]{1,0:T(8,128)}, f32[8192,3]{1,0:T(8,128)}) fusion(f32[8192,8]{1,0:T(8,128)} %bitcast.99), kind=kLoop, calls=%fused_computation.111 | loop fusion | bytes 589824 | tf_op jit(solution)/shard_map/transpose | solution.py:18
  205.8 7.6 %gather_fusion.5 = f32[2048,3]{1,0:T(8,128)S(1)} fusion(f32[3,8192]{0,1:T(8,128)} %get-tuple-element.33, s32[2048]{0:T(1024)S(1)} %fusion.27), kind=kCustom, calls=%fused_computation.6.clone | custom fusion | bytes 57344 | tf_op jit(solution)/shard_map/jit(_take)/gather | solution.py:175
  213.4 7.6 %gather_fusion.1 = f32[2048,3]{1,0:T(8,128)S(1)} fusion(f32[3,8192]{0,1:T(8,128)} %get-tuple-element.33, s32[2048]{0:T(1024)S(1)} %fusion.26), kind=kCustom, calls=%fused_computation.1.clone | custom fusion | bytes 57344 | tf_op jit(solution)/shard_map/jit(_take)/gather | solution.py:175
  221.1 9.8 %gather_fusion.3 = f32[2048,3]{1,0:T(8,128)} fusion(f32[3,8192]{0,1:T(8,128)} %get-tuple-element.34, s32[2048]{0:T(1024)S(1)} %fusion.26), kind=kCustom, calls=%fused_computation.5.clone | custom fusion | bytes 57344 | tf_op jit(solution)/shard_map/jit(_take)/gather | solution.py:177
  230.8 9.9 %gather_fusion.7 = f32[2048,3]{1,0:T(8,128)} fusion(f32[3,8192]{0,1:T(8,128)} %get-tuple-element.34, s32[2048]{0:T(1024)S(1)} %fusion.27), kind=kCustom, calls=%fused_computation.7.clone | custom fusion | bytes 57344 | tf_op jit(solution)/shard_map/jit(_take)/gather | solution.py:177
  240.7 1.5 dynamic-slice_reduce_fusion
  242.4 1.3 dynamic-slice_bitcast_fusion
  243.7 0.8 slice_reduce_fusion.14
  244.5 0.8 slice_reduce_fusion.17
  245.3 1.6 select_bitcast_fusion.3
  246.9 1.4 slice_reduce_fusion.11
  248.3 1.6 select_bitcast_fusion.1
  249.9 1.4 slice_reduce_fusion.5
  251.5 1.4 slice_reduce_fusion.2
  252.9 1.4 slice_reduce_fusion.8
  254.5 33.1 %fusion.5 = (f32[1024,4,256]{0,2,1:T(8,128)}, f32[1024,4,256]{0,2,1:T(8,128)}) fusion(f32[1024]{0:T(1024)S(1)} %bitcast.116, f32[1024]{0:T(1024)S(1)} %bitcast.119, f32[1024]{0:T(1024)S(1)} %bitcast.113, f32[4,256]{1,0:T(4,128)S(1)} %mul.505, f32[4,256]{1,0:T(4,128)S(1)} %mul.502, f32[4,256]{1,0:T(4,128)S(1)} %mul.499, f32[4,256]{1,0:T(4,128)S(1)} %add.256, ...), kind=kLoop, calls=%fused_computation.25 | loop fusion | flops 37748736 | bytes 8445952 | tf_op jit(solution)/shard_map/convert_element_type | solution.py:76
  287.6 1.6 copy.27
  289.2 8.6 %reshape.627 = bf16[32,131072]{1,0:T(8,128)(2,1)} reshape(bf16[16,2,131072]{2,1,0:T(2,128)(2,1)} %all-to-all-done.2) | data formatting | bytes 16777216 | tf_op jit(solution)/shard_map/reshape | solution.py:159
  297.9 4.7 convolution_convert_fusion.1
  302.6 1.6 fusion.33
  304.2 2.2 reshape.729
  306.4 2.5 reshape.728
  309.0 3.0 fusion.13
  312.1 1.3 fusion.16
  313.4 0.9 copy-done
  314.2 33.8 %fusion.2 = f32[1024,512]{0,1:T(8,128)S(1)} fusion(f32[1024,4,256]{0,2,1:T(8,128)S(1)} %copy-done, bf16[4,512,512]{1,2,0:T(8,128)(2,1)S(1)} %bitcast.106, f32[4,512]{1,0:T(4,128)S(1)} %mul.529, f32[4,512]{1,0:T(4,128)S(1)} %mul.526, f32[4,512]{1,0:T(4,128)S(1)} %mul.523, f32[4,512]{1,0:T(4,128)S(1)} %add.263, f32[4,512]{1,0:T(4,128)S(1)} %sub.262, ...), kind=kOutput, calls=%fused_computation.16 | convolution fusion | flops 2186805248 | bytes 8466432 | tf_op jit(solution)/shard_map/gax,axy->gay/dot_general | solution.py:72
  348.1 0.1 bitcast_reduce_fusion
  348.2 33.6 %fusion = f32[1024,512]{0,1:T(8,128)S(1)} fusion(f32[1024,4,256]{0,2,1:T(8,128)S(1)} %copy-done.1, bf16[4,512,512]{1,2,0:T(8,128)(2,1)S(1)} %bitcast.105, f32[4,512]{1,0:T(4,128)S(1)} %mul.484, f32[4,512]{1,0:T(4,128)S(1)} %mul.481, f32[4,512]{1,0:T(4,128)S(1)} %mul.478, f32[4,512]{1,0:T(4,128)S(1)} %add.248, f32[4,512]{1,0:T(4,128)S(1)} %sub.235, ...), kind=kOutput, calls=%fused_computation.14 | convolution fusion | flops 2186805248 | bytes 8466432 | tf_op jit(solution)/shard_map/gax,axy->gay/dot_general | solution.py:72
  381.9 0.1 bitcast_reduce_fusion.1
  382.0 0.2 mul.513
  382.3 1.6 fusion.1
  383.9 33.7 %convolution_convert_fusion.3 = bf16[4,512,512]{1,2,0:T(8,128)(2,1)S(1)} fusion(bf16[1024,4,512]{0,2,1:T(8,128)(2,1)S(1)} %fusion.1, f32[4,512]{1,0:T(4,128)S(1)} %mul.484, f32[4,512]{1,0:T(4,128)S(1)} %mul.481, f32[4,512]{1,0:T(4,128)S(1)} %mul.478, f32[4,512]{1,0:T(4,128)S(1)} %add.248, f32[4,512]{1,0:T(4,128)S(1)} %sub.235, f32[1024]{0:T(1024)S(1)} %bitcast.124, ...), kind=kOutput, calls=%fused_computation.38 | convolution fusion | flops 2184183808 | bytes 6369280 | tf_op jit(solution)/shard_map/gax,gay->axy/dot_general | solution.py:85
  417.6 1.2 fusion.9
  418.9 0.2 mul.550
  419.1 1.6 fusion.3
  420.7 42.9 %convolution_convert_fusion.2 = bf16[4,512,512]{1,2,0:T(8,128)(2,1)S(1)} fusion(bf16[1024,4,512]{0,2,1:T(8,128)(2,1)S(1)} %fusion.3, f32[4,512]{1,0:T(4,128)S(1)} %mul.529, f32[4,512]{1,0:T(4,128)S(1)} %mul.526, f32[4,512]{1,0:T(4,128)S(1)} %mul.523, f32[4,512]{1,0:T(4,128)S(1)} %add.263, f32[4,512]{1,0:T(4,128)S(1)} %sub.262, f32[1024]{0:T(1024)S(1)} %bitcast.118, ...), kind=kOutput, calls=%fused_computation.37 | convolution fusion | flops 2184183808 | bytes 6369280 | tf_op jit(solution)/shard_map/gax,gay->axy/dot_general | solution.py:85
  463.6 1.3 fusion.21
  464.9 0.2 copy.30
  465.1 0.2 copy.31
  465.4 33.3 %all_to_all.28 = bf16[16,64,2,512]{3,1,2,0:T(8,128)(2,1)S(1)} all-to-all(bf16[16,64,2,512]{3,1,2,0:T(8,128)(2,1)S(1)} %copy.31), channel_id=1, replica_groups=mesh['row'=8,'col'=16] {'col'}, dimensions={0} | all-to-all | bytes 4194304 | tf_op jit(solution)/shard_map/all_to_all | solution.py:48
  498.6 0.3 convert_reduce_fusion
  498.9 0.9 copy.33
  (73 shorter events, 0.9 us)
Async XLA Ops:
  0.0 40.0 %copy-start.11 = (f32[64]{0:T(128)S(1)}, f32[64]{0:T(128)}, u32[]{:S(2)}) copy-start(f32[64]{0:T(128)} %param.19) | copy-start | bytes 772
  0.0 40.0 %copy-start.9 = (f32[3,64]{1,0:T(4,128)S(1)}, f32[3,64]{1,0:T(4,128)}, u32[]{:S(2)}) copy-start(f32[3,64]{1,0:T(4,128)} %param.18) | copy-start | bytes 2308
  0.0 40.0 %copy-start.12 = (f32[64]{0:T(128)S(1)}, f32[64]{0:T(128)}, u32[]{:S(2)}) copy-start(f32[64]{0:T(128)} %param.17) | copy-start | bytes 772
  0.0 40.0 %copy-start.10 = (f32[3,64]{1,0:T(4,128)S(1)}, f32[3,64]{1,0:T(4,128)}, u32[]{:S(2)}) copy-start(f32[3,64]{1,0:T(4,128)} %param.16) | copy-start | bytes 2308
  36.1 96.3 %all-to-all-start.3 = ((bf16[16,2,64,512]{3,2,1,0:T(8,128)(2,1)}), bf16[16,2,64,512]{3,2,1,0:T(8,128)(2,1)S(1)}, u32[]{:S(2)}, u32[]{:S(2)}) async-start(bf16[16,2,64,512]{3,2,1,0:T(8,128)(2,1)} %broadcast_in_dim.17), calls=%async_computation.3 | async-start | bytes 4194304 | tf_op jit(solution)/shard_map/all_to_all | solution.py:31
  132.4 1.4 copy-start.3
  133.8 155.5 %all-to-all-start.2 = ((bf16[16,2,131072]{2,1,0:T(2,128)(2,1)}), bf16[16,2,131072]{2,1,0:T(2,128)(2,1)}, u32[]{:S(2)}, u32[]{:S(2)}) async-start(bf16[16,2,131072]{2,1,0:T(2,128)(2,1)} %reshape.626), calls=%async_computation.2 | async-start | bytes 16777216 | tf_op jit(solution)/shard_map/all_to_all | solution.py:156
  249.9 4.5 copy-start.7
  249.9 4.5 copy-start.8
  249.9 4.6 copy-start.6
  254.5 33.1 %copy-start.4 = (bf16[16,2,64,512]{3,2,1,0:T(8,128)(2,1)S(1)}, bf16[16,2,64,512]{3,2,1,0:T(8,128)(2,1)}, u32[]{:S(2)}) copy-start(bf16[16,2,64,512]{3,2,1,0:T(8,128)(2,1)} %copy-done.3) | copy-start | bytes 6291460
  309.0 3.1 copy-start.2
  309.0 3.1 copy-start.5
  312.0 2.2 copy-start
  314.2 34.0 %copy-start.1 = (f32[1024,4,256]{0,2,1:T(8,128)S(1)}, f32[1024,4,256]{0,2,1:T(8,128)}, u32[]{:S(2)}) copy-start(f32[1024,4,256]{0,2,1:T(8,128)} %get-tuple-element.40) | copy-start | bytes 12582916
where the time goes:
time: 507 us; the launch traced here: 500 us
  matrix products  161 us (32%)
  local copies, waits for them, and re-layouts  148 us (29%)
  blocking collectives  137 us (27%)
  other arithmetic  44 us (9%)
  starting transfers between devices  8.98 us (2%)
    dot_general x2, matrix products, batch_response(): jnp.einsum('gax,gay->axy', col_phi, scaled, preferred_element_type=jnp.fl...  76.7 us
    all_gather x1, blocking collectives, rows_first(): lax.all_gather(both, axis, axis=0, tiled=True)  73.7 us
    dot_general x2, matrix products, batch_response(): jnp.einsum('gax,axy->gay', col_phi, pair_tiles, preferred_element_type=jn...  67.5 us
    all_to_all x1, blocking collectives, sum_at_owner(): tiles = lax.all_to_all(split_up(value, dim, size), axis, 0, 0, tiled=True)  33.3 us
    convert_element_type x1, other arithmetic, batch_response(): row_values.astype(jnp.float32).reshape(npoints, row_tiles, 1, tile_size)  33.1 us
    gather x2, local copies, waits for them, and re-layouts, per_device(): jnp.take(all_phases, index_now)  23.6 us
    gather x2, local copies, waits for them, and re-layouts, per_device(): jnp.take(all_exponents, index_now)  23.6 us
    gather x2, local copies, waits for them, and re-layouts, per_device(): jnp.take(all_waves, index_now, axis=1)  19.6 us
  transfers between devices with their start and end apart: 2, of which 0 were waited for; matrix products, arithmetic and copies ran while one was open for 34% of the time, Pallas kernels for 0%

commit v1 on v0

v1 whole, which is shorter than its diff:
```python
import functools
import math

import jax
import jax.numpy as jnp
from jax import lax
from jax.experimental import pallas as pl
from jax.experimental.pallas import tpu as pltpu
from jax.sharding import PartitionSpec as P

BF = jnp.bfloat16
F32 = jnp.float32
MESH = pl.DeviceIdType.MESH
FULL = slice(None)
EXCHANGE_COEF = 0.75 * (3.0 / 3.141592653589793) ** (1.0 / 3.0)
S0, S1, S2, S3 = 6.283164044302474, -41.33714237110029, 81.34076888766828, -70.99343327209985
D0, D1, D2 = S0 / S3, S1 / S3, S2 / S3
LOG_S = math.log2(-S3)
LOG2E = math.log2(math.e)
TURN = 1.0 / (2.0 * math.pi)
GRID = 1024
CHUNK = 256


class Net:
    def __init__(self, send_sem, recv_sem):
        self.row, self.col = lax.axis_index("row"), lax.axis_index("col")
        self.pos = {"x": self.col // 4, "y": self.col % 4, "z": self.row // 2}
        self.core = self.row % 2
        self.send_sem, self.recv_sem = send_sem, recv_sem
        self.count = 0
        self.sent = []

    def at(self, dim, step):
        return lax.rem(self.pos[dim] + (step + 4), 4)

    def chip(self, dim, step):
        p = dict(self.pos)
        p[dim] = self.at(dim, step)
        return (p["z"] * 2 + self.core, p["x"] * 4 + p["y"])

    def partner(self):
        return (self.row + 1 - 2 * self.core, self.col)

    def copy(self, i, src, dst, device):
        return pltpu.make_async_remote_copy(
            src_ref=src,
            dst_ref=dst,
            send_sem=self.send_sem.at[i],
            recv_sem=self.recv_sem.at[i],
            device_id=device,
            device_id_type=MESH,
        )

    def send(self, src, dst, device):
        i = self.count
        self.count += 1
        c = self.copy(i, src, dst, device)
        c.start()
        self.sent.append(c)
        return i

    def arrived(self, i, dst):
        self.copy(i, dst, dst, self.partner()).wait_recv()

    def drain(self):
        for c in self.sent:
            c.wait_send()
        self.sent = []


def barrier(net):
    sem = pltpu.get_barrier_semaphore()
    peers = [net.partner()] + [net.chip(d, s) for d in "xyz" for s in (1, -1, 2)]
    for p in peers:
        pl.semaphore_signal(sem, inc=1, device_id=p, device_id_type=MESH)
    pl.semaphore_wait(sem, len(peers))


class Gather:
    def __init__(self, net, view, order, direct, forward=1):
        self.net, self.view, self.order, self.direct, self.forward = net, view, order, direct, forward
        self.phase = 0
        self.shared = []

    def index(self, **over):
        idx = dict(self.net.pos)
        for d in self.order[: self.phase]:
            idx[d] = FULL
        idx.update(over)
        return idx

    def start(self):
        net, d = self.net, self.order[self.phase]
        mine = self.view(self.index(), net.core)
        self.ids = {}
        for s in (1, -1) + ((2,) if self.direct[self.phase] else ()):
            self.ids[-s if s != 2 else 2] = net.send(mine, mine, net.chip(d, s))

    def take(self, s):
        net, d = self.net, self.order[self.phase]
        b = self.view(self.index(**{d: net.at(d, s)}), net.core)
        net.arrived(self.ids[s], b)
        if not self.direct[self.phase] and s == -self.forward:
            self.ids[2] = net.send(b, b, net.chip(d, self.forward))

    def step(self):
        for s in (-self.forward, self.forward, 2):
            self.take(s)
        self.phase += 1
        if self.phase < len(self.order):
            self.start()

    def share(self, s=None):
        d = self.order[self.phase]
        idx = self.index() if s is None else self.index(**{d: self.net.at(d, s)})
        b = self.view(idx, self.net.core)
        self.shared.append((self.net.send(b, b, self.net.partner()), idx))

    def get_shared(self):
        for i, idx in self.shared:
            self.net.arrived(i, self.view(idx, 1 - self.net.core))


def dot(a, b, ca=1, cb=0):
    return lax.dot_general(a, b, (((ca,), (cb,)), ((), ())), preferred_element_type=F32)


def splits(x):
    hi = x.astype(BF)
    rest = x - hi.astype(F32)
    mid = rest.astype(BF)
    return hi, mid, (rest - mid.astype(F32)).astype(BF)


def func_features(g):
    row = lax.broadcasted_iota(jnp.int32, g.shape, 0)
    ph = jnp.where((row >= 3) & (row != 6), g * TURN, 0.0)
    ex = g[6:7] * LOG2E
    c2 = g[0:1] * g[0:1] + g[1:2] * g[1:2] + g[2:3] * g[2:3]
    ee = jnp.where(row < 3, 2.0 * ex * g, jnp.where(row == 6, -ex, jnp.where(row == 7, LOG_S - ex * c2, 0.0)))
    hi, mid, lo = splits(jnp.concatenate([ph, ee], axis=0))
    return jnp.concatenate([hi, hi, hi, mid, mid, mid, lo, lo], axis=0)


def point_features(p):
    p0, p1, p2 = p[0:1], p[1:2], p[2:3]
    row = lax.broadcasted_iota(jnp.int32, (8, p.shape[1]), 0)
    rows = lambda *pairs: functools.reduce(lambda acc, rv: jnp.where(row == rv[0], rv[1], acc), pairs, jnp.zeros(row.shape, F32))
    ph = rows((3, p0), (4, p1), (5, p2), (7, 1.0))
    ee = rows((0, p0), (1, p1), (2, p2), (6, p0 * p0 + p1 * p1 + p2 * p2), (7, 1.0))
    zero = jnp.zeros_like(ph)
    out = []
    for parts in ([ph, zero], [zero, ee]):
        hi, mid, lo = splits(jnp.concatenate(parts, axis=0))
        out.append(jnp.concatenate([hi, mid, lo, hi, mid, lo, hi, mid], axis=0))
    return out


def basis(phase, exponent):
    r = phase - lax.round(phase, lax.RoundingMethod.TO_NEAREST_EVEN)
    z = jnp.abs(r) - 0.25
    y = z * z
    return (jnp.exp2(exponent) * (z * (((y + D2) * y + D1) * y + D0))).astype(BF)


def chunks():
    return [pl.ds(c, CHUNK) for c in range(0, GRID, CHUNK)]


def fused(
    occ, tri, cen, wav, exo, pha, pts, den, wts, src, out,
    O, T, G, par, FT, FR, PT, PP, phiR, phiC, B, rho, vk, Rb, H, A, S, A2,
    send_sem, recv_sem, local_sem,
):
    net = Net(send_sem, recv_sem)
    x, y, z, core = net.pos["x"], net.pos["y"], net.pos["z"], net.core
    local = [
        pltpu.make_async_copy(occ, O.at[x, y, z, core], local_sem.at[0]),
        pltpu.make_async_copy(tri, T.at[:, x, y], local_sem.at[1]),
    ]
    for c in local:
        c.start()
    par[...] = jnp.zeros_like(par)
    par[0:3, 0:64] = cen[...]
    par[3:6, 0:64] = wav[...]
    par[6:7, 0:64] = exo[...]
    par[7:8, 0:64] = pha[...]
    G[z, core, x, y] = par[...]
    barrier(net)
    for c in local:
        c.wait()

    gp = Gather(net, lambda i, c: G.at[i["z"], c, i["x"], i["y"]], "xyz", (1, 1, 1))
    go = [
        Gather(net, lambda i, c, p=p: O.at[i["x"], i["y"], i["z"], c, p], o, (1, 1, 0), f)
        for p, (o, f) in enumerate((("xyz", 1), ("yxz", -1), ("zxy", -1), ("zyx", -1)))
    ]
    gt = [Gather(net, lambda i, c, k=k: T.at[k, i["x"], i["y"]], o, (1, 0), -1) for k, o in enumerate(("xy", "yx"))]
    gp.start()
    for g in go + gt:
        g.start()

    for b in range(2):
        f = point_features(pts[b])
        for i in range(2):
            PT[b, i] = f[i]
            PP[b, i] = f[i].T
    gp.step()
    for g in gt + go:
        g.step()
    gp.step()
    gp.share()

    def tile_features(zz, cc, xx):
        return func_features(jnp.concatenate([G[zz, cc, xx, i][:, :64] for i in range(4)], axis=1))

    for a in range(4):
        FR[a] = tile_features(z, core, a).T

    def rows(lo, hi):
        def body(i, _):
            b, a = i // 4, i % 4
            for sl in chunks():
                phiR[b, a, :, sl] = basis(dot(FR[a], PT[b, 0, :, sl]), dot(FR[a], PT[b, 1, :, sl]))
            return 0

        lax.fori_loop(lo, hi, body, 0)

    def cols(lo, hi):
        def body(i, _):
            b, j = i // 8, i % 8
            f = FT[src[b, j, 0] * 2 + j % 2]
            for sl in chunks():
                phiC[b, j, sl, :] = basis(dot(PP[b, 0, sl], f), dot(PP[b, 1, sl], f))
            return 0

        lax.fori_loop(lo, hi, body, 0)

    rows(0, 2)
    for g in go:
        g.step()
        g.share()
    rows(2, 5)
    for s in (1, -1, 2):
        gp.take(s)
        gp.share(s)
    rows(5, 8)
    for g in gt:
        g.take(-g.forward)
    for g in go:
        g.take(-g.forward)
        g.share(-g.forward)
    gp.get_shared()

    def all_features(t, _):
        FT[t] = tile_features(t // 8, (t // 4) % 2, t % 4)
        return 0

    lax.fori_loop(0, 32, all_features, 0)
    cols(0, 5)
    for g in go:
        g.take(g.forward)
        g.share(g.forward)
    cols(5, 10)
    for g in gt:
        g.take(g.forward)
        g.take(2)
    cols(10, 16)
    for g in go:
        g.take(2)
        g.share(2)
    for g in go:
        g.get_shared()

    def half(i, _):
        b, a = i // 4, i % 4
        o = []
        for j in range(2):
            s = src[b, 2 * a + j, 0]
            o.append(O[s // 4, s % 4, 2 * j : 2 * j + 2].reshape(256, 512))
        for sl in chunks():
            B[i, sl, :] = (dot(phiC[b, 2 * a, sl, :], o[0]) + dot(phiC[b, 2 * a + 1, sl, :], o[1])).astype(BF)
        return 0

    lax.fori_loop(0, 8, half, 0)

    rho[...] = jnp.zeros_like(rho)

    def densities(i, _):
        b, a = i // 4, i % 4
        for sl in chunks():
            bb = B[i, sl, :]
            phi = phiR[b, a, :, sl].astype(F32)
            for k in range(2):
                cc = dot(T[k, a].reshape(256, 512), bb, 1, 1)
                rho[b, k : k + 1, sl] += jnp.sum(cc * phi, axis=0, keepdims=True)
        return 0

    lax.fori_loop(0, 8, densities, 0)
    for b in range(2):
        f = wts[b : b + 1, :] * (-(4.0 / 9.0) * EXCHANGE_COEF * jnp.exp(-(2.0 / 3.0) * jnp.log(den[b : b + 1, :])))
        for k in range(2):
            vk[b, k : k + 1, :] = f * rho[b, k : k + 1, :]

    def tile(k, a):
        acc = None
        for b in range(2):
            sc = (phiR[b, a].astype(F32) * vk[b, k : k + 1, :]).astype(BF)
            d = dot(sc, B[b * 4 + a])
            acc = d if acc is None else acc + d
        Rb[k, a] = acc.astype(BF).reshape(4, 64, 512)

    dims = ("x", "y")

    def chunk(k, c, half=FULL):
        return Rb.at[0, c, half] if k == 0 else Rb.at[1, half, c]

    lows, highs = pl.ds(0, 2), pl.ds(2, 2)
    ids = [{}, {}]

    def opposite(k):
        d = dims[k]
        c = net.at(d, 2)
        ids[k]["h0"] = net.send(chunk(k, c, lows), H.at[k, 0], net.chip(d, 1))
        ids[k]["h1"] = net.send(chunk(k, c, highs), H.at[k, 1], net.chip(d, -1))

    def neighbours(k):
        d = dims[k]
        for n, (s, hs) in enumerate(((1, lows), (-1, highs))):
            c = net.at(d, s)
            net.arrived(ids[k][f"h{n}"], H.at[k, n])
            part = chunk(k, c, hs)
            part[...] = (part[...].astype(F32) + H[k, n].astype(F32)).astype(BF)
            ids[k][f"a{n}"] = net.send(chunk(k, c), A.at[k, n], net.chip(d, s))

    def second(k):
        d, e = dims[k], dims[1 - k]
        for n in range(2):
            net.arrived(ids[k][f"a{n}"], A.at[k, n])
        total = chunk(k, net.pos[d])[...].astype(F32) + A[k, 0].astype(F32) + A[k, 1].astype(F32)
        S[k] = total.astype(BF)
        for n, s in enumerate((2, 1, -1)):
            ids[k][f"s{n}"] = net.send(S.at[k, net.at(e, s)], A2.at[k, n], net.chip(e, s))

    def finish(k):
        total = S[k, net.pos[dims[1 - k]]].astype(F32)
        for n in range(3):
            net.arrived(ids[k][f"s{n}"], A2.at[k, n])
            total = total + A2[k, n].astype(F32)
        out[:, k, :] = total

    def tiles_1(a, _):
        tile(1, a)
        return 0

    lax.fori_loop(0, 4, tiles_1, 0)
    opposite(1)
    tile(0, net.at("x", 2))
    opposite(0)
    tile(0, net.at("x", 1))
    tile(0, net.at("x", -1))
    neighbours(1)
    neighbours(0)
    tile(0, net.pos["x"])
    second(1)
    second(0)
    finish(1)
    finish(0)
    net.drain()


SEMS = 140


def per_device(tri, occ, cen, exo, wav, pha, pts, den, wts, src):
    vmem, hbm = pl.BlockSpec(memory_space=pltpu.VMEM), pl.BlockSpec(memory_space=pl.ANY)
    return pl.pallas_call(
        fused,
        out_shape=jax.ShapeDtypeStruct((64, 2, 512), F32),
        in_specs=[hbm, hbm] + [vmem] * 7 + [pl.BlockSpec(memory_space=pltpu.SMEM)],
        out_specs=vmem,
        scratch_shapes=[
            pltpu.VMEM((4, 4, 4, 2, 4, 16, 512), BF),
            pltpu.VMEM((2, 4, 4, 64, 512), BF),
            pltpu.VMEM((4, 2, 4, 4, 8, 128), F32),
            pltpu.VMEM((8, 128), F32),
            pltpu.VMEM((32, 128, 256), BF),
            pltpu.VMEM((4, 256, 128), BF),
            pltpu.VMEM((2, 2, 128, GRID), BF),
            pltpu.VMEM((2, 2, GRID, 128), BF),
            pltpu.VMEM((2, 4, 256, GRID), BF),
            pltpu.VMEM((2, 8, GRID, 256), BF),
            pltpu.VMEM((8, GRID, 512), BF),
            pltpu.VMEM((2, 2, GRID), F32),
            pltpu.VMEM((2, 2, GRID), F32),
            pltpu.VMEM((2, 4, 4, 64, 512), BF),
            pltpu.VMEM((2, 2, 2, 64, 512), BF),
            pltpu.VMEM((2, 2, 4, 64, 512), BF),
            pltpu.VMEM((2, 4, 64, 512), BF),
            pltpu.VMEM((2, 3, 64, 512), BF),
            pltpu.SemaphoreType.DMA((SEMS,)),
            pltpu.SemaphoreType.DMA((SEMS,)),
            pltpu.SemaphoreType.DMA((2,)),
        ],
        compiler_params=pltpu.CompilerParams(collective_id=0, has_side_effects=True, vmem_limit_bytes=62 * 2**20),
        name="fused",
    )(occ.reshape(4, 16, 512), tri, cen, wav, exo.reshape(1, 64), pha.reshape(1, 64), pts, den, wts, src)


def solution(mesh):
    both = ("row", "col")
    in_specs = (
        P(None, both, None),
        P(("col", "row"), None),
        P(None, both),
        P(both),
        P(None, both),
        P(both),
        P(both, None, None),
        P(both, None),
        P(both, None),
        P(both, None, None),
    )
    return jax.shard_map(per_device, mesh=mesh, in_specs=in_specs, out_specs=P(both, None, None), check_vma=False)
```

time: 507 us -> 91.8 us (0.18); the launches traced: 500 us -> 91.5 us
  matrix products: 161 us -> 0 us
  local copies, waits for them, and re-layouts: 148 us -> 4.39 us
  blocking collectives: 137 us -> 0 us
  Pallas kernels: 0 us -> 87.1 us
  other arithmetic: 44 us -> 0 us
  starting transfers between devices: 8.98 us -> 0 us
    dot_general x10 -> x0, matrix products: 161 us -> none  [the longest x2 76.7 us: batch_response(): jnp.einsum('gax,gay->axy', col_phi, scaled, preferred_element_type=jnp.fl...]
    pallas_call x0 -> x1, Pallas kernels: none -> 87.1 us  [per_device(): pl.pallas_call(fused, out_shape=jax.ShapeDtypeStruct((64, 2, 512), F32),...]
    gather x8 -> x0, local copies, waits for them, and re-layouts: 82 us -> none  [the longest x2 23.6 us: per_device(): jnp.take(all_phases, index_now)]
    all_gather x1 -> x0, blocking collectives: 73.7 us -> none  [rows_first(): lax.all_gather(both, axis, axis=0, tiled=True)]
    all_to_all x3 -> x0, blocking collectives: 63.6 us -> none  [the longest x1 33.3 us: sum_at_owner(): tiles = lax.all_to_all(split_up(value, dim, size), axis, 0, 0, tiled=True)]
    convert_element_type x4 -> x0, other arithmetic: 36.3 us -> none  [the longest x1 33.1 us: batch_response(): row_values.astype(jnp.float32).reshape(npoints, row_tiles, 1, tile_size)]
    reshape x4 -> x0, local copies, waits for them, and re-layouts: 18.2 us -> none  [the longest x1 9.37 us: per_device(): outgoing_rows = jnp.dot(col_hot, col_factor.reshape(tiles_col, TB * orbit...]
    slice x9 -> x0, local copies, waits for them, and re-layouts: 17.9 us -> none  [the longest x1 8.96 us: rows_first(): slab = filled[:, at:at + t[0].size].reshape(-1, *t.shape[1:])]
  transfers between devices with their start and end apart: 2 -> 0, of which waited for: 0 -> 0; matrix products, arithmetic and copies ran while one was open for 34% -> 0% of each run, Pallas kernels for 0% -> 0%
where the time goes in v1:
time: 91.8 us; the launch traced here: 91.5 us
  Pallas kernels  87.1 us (95%)
  local copies, waits for them, and re-layouts  4.39 us (5%)
    pallas_call x1, Pallas kernels, per_device(): pl.pallas_call(fused, out_shape=jax.ShapeDtypeStruct((64, 2, 512), F32),...  87.1 us
    unnamed x5, local copies, waits for them, and re-layouts  4.39 us

profile of v1, /device:TPU:1, one launch (start us, length us, event | category | flops | bytes accessed | tf_op | source)
XLA Modules:
  0.0 91.5 jit_solution(2658544802307416017)
XLA Ops:
  0.0 0.0 copy-start
  0.0 0.7 copy-done
  0.7 0.7 copy.12.src
  1.4 1.4 %copy.11.pts = f32[2,3,1024]{2,1,0:T(4,128)} copy(f32[2,3,1024]{2,0,1:T(2,128)} %param.16) | data formatting | bytes 49152 | tf_op args[6]
  2.7 87.1 %fused.1 = f32[64,2,512]{2,1,0:T(2,128)} custom-call(bf16[4,16,512]{2,1,0:T(8,128)(2,1)} %bitcast.3, bf16[2,64,512]{2,1,0:T(8,128)(2,1)} %tri.1, f32[3,64]{1,0:T(4,128)} %cen.1, f32[3,64]{1,0:T(4,128)} %wav.1, f32[1,64]{1,0:T(1,128)} %bitcast.4, f32[1,64]{1,0:T(1,128)} %bitcast.5, f32[2,3,1024]{2,1,0:T(4,128)} %copy.11.pts, f32[2,1024]{1,0:T(2,128)} %den.1, ...), custom_call_target="tpu_custom_call" | custom-call | tf_op jit(solution)/shard_map/fused/pallas_call | solution.py:378
  89.9 1.7 %copy.14 = f32[64,2,512]{2,1,0:T(2,128)} copy(f32[64,2,512]{2,1,0:T(2,128)} %fused.1) | data formatting | bytes 524288
Async XLA Ops:
  0.0 0.7 copy-start

commit v2 on v1

--- a/solution.py
+++ b/solution.py
@@ -144,8 +144,8 @@
 
 
 def point_features(p):
-    p0, p1, p2 = p[0:1], p[1:2], p[2:3]
-    row = lax.broadcasted_iota(jnp.int32, (8, p.shape[1]), 0)
+    p0, p1, p2 = p
+    row = lax.broadcasted_iota(jnp.int32, (8, p0.shape[1]), 0)
     rows = lambda *pairs: functools.reduce(lambda acc, rv: jnp.where(row == rv[0], rv[1], acc), pairs, jnp.zeros(row.shape, F32))
     ph = rows((3, p0), (4, p1), (5, p2), (7, 1.0))
     ee = rows((0, p0), (1, p1), (2, p2), (6, p0 * p0 + p1 * p1 + p2 * p2), (7, 1.0))
@@ -202,12 +202,12 @@
         g.start()
 
     for b in range(2):
-        f = point_features(pts[b])
+        f = point_features([pts[i, b : b + 1, :] for i in range(3)])
         for i in range(2):
             PT[b, i] = f[i]
             PP[b, i] = f[i].T
     gp.step()
-    for g in gt + go:
+    for g in go + gt:
         g.step()
     gp.step()
     gp.share()
@@ -230,7 +230,7 @@
     def cols(lo, hi):
         def body(i, _):
             b, j = i // 8, i % 8
-            f = FT[src[b, j, 0] * 2 + j % 2]
+            f = FT[src[b, 0, j] * 2 + j % 2]
             for sl in chunks():
                 phiC[b, j, sl, :] = basis(dot(PP[b, 0, sl], f), dot(PP[b, 1, sl], f))
             return 0
@@ -277,7 +277,7 @@
         b, a = i // 4, i % 4
         o = []
         for j in range(2):
-            s = src[b, 2 * a + j, 0]
+            s = src[b, 0, 2 * a + j]
             o.append(O[s // 4, s % 4, 2 * j : 2 * j + 2].reshape(256, 512))
         for sl in chunks():
             B[i, sl, :] = (dot(phiC[b, 2 * a, sl, :], o[0]) + dot(phiC[b, 2 * a + 1, sl, :], o[1])).astype(BF)
@@ -405,7 +405,7 @@
         ],
         compiler_params=pltpu.CompilerParams(collective_id=0, has_side_effects=True, vmem_limit_bytes=62 * 2**20),
         name="fused",
-    )(occ.reshape(4, 16, 512), tri, cen, wav, exo.reshape(1, 64), pha.reshape(1, 64), pts, den, wts, src)
+    )(occ.reshape(4, 16, 512), tri, cen, wav, exo.reshape(1, 64), pha.reshape(1, 64), pts.transpose(1, 0, 2), den, wts, src.transpose(0, 2, 1))
 
 
 def solution(mesh):

time: 91.8 us -> 84.3 us (0.918)
  Pallas kernels: 87.1 us -> 82.4 us
  local copies, waits for them, and re-layouts: 4.39 us -> 1.67 us
    pallas_call x1, Pallas kernels: 87.1 us -> 82.4 us  [per_device(): pl.pallas_call(fused, out_shape=jax.ShapeDtypeStruct((64, 2, 512), F32),...]
    unnamed x5 -> x1, local copies, waits for them, and re-layouts: 4.39 us -> 1.67 us
where the time goes in v2:
time: 84.3 us; the launch traced here: 84.1 us
  Pallas kernels  82.4 us (98%)
  local copies, waits for them, and re-layouts  1.67 us (2%)
    pallas_call x1, Pallas kernels, per_device(): pl.pallas_call(fused, out_shape=jax.ShapeDtypeStruct((64, 2, 512), F32),...  82.4 us

profile of v2, /device:TPU:1, one launch (start us, length us, event | category | flops | bytes accessed | tf_op | source)
XLA Modules:
  0.0 84.1 jit_solution(4201514862525223360)
XLA Ops:
  0.0 82.4 %fused.1 = f32[64,2,512]{2,1,0:T(2,128)} custom-call(bf16[4,16,512]{2,1,0:T(8,128)(2,1)} %bitcast.7, bf16[2,64,512]{2,1,0:T(8,128)(2,1)} %tri.1, f32[3,64]{1,0:T(4,128)} %cen.1, f32[3,64]{1,0:T(4,128)} %wav.1, f32[1,64]{1,0:T(1,128)} %bitcast.10, f32[1,64]{1,0:T(1,128)} %bitcast.11, f32[3,2,1024]{2,1,0:T(2,128)} %bitcast.8, f32[2,1024]{1,0:T(2,128)} %den.1, ...), custom_call_target="tpu_custom_call" | custom-call | tf_op jit(solution)/shard_map/fused/pallas_call | solution.py:378
  82.4 1.7 %copy.13 = f32[64,2,512]{2,1,0:T(2,128)} copy(f32[64,2,512]{2,1,0:T(2,128)} %fused.1) | data formatting | bytes 524288

commit v3 on v2

--- a/solution.py
+++ b/solution.py
@@ -246,11 +246,11 @@
         gp.take(s)
         gp.share(s)
     rows(5, 8)
-    for g in gt:
-        g.take(-g.forward)
     for g in go:
         g.take(-g.forward)
         g.share(-g.forward)
+    for g in gt:
+        g.take(-g.forward)
     gp.get_shared()
 
     def all_features(t, _):
@@ -262,11 +262,7 @@
     for g in go:
         g.take(g.forward)
         g.share(g.forward)
-    cols(5, 10)
-    for g in gt:
-        g.take(g.forward)
-        g.take(2)
-    cols(10, 16)
+    cols(5, 16)
     for g in go:
         g.take(2)
         g.share(2)
@@ -283,21 +279,33 @@
             B[i, sl, :] = (dot(phiC[b, 2 * a, sl, :], o[0]) + dot(phiC[b, 2 * a + 1, sl, :], o[1])).astype(BF)
         return 0
 
-    lax.fori_loop(0, 8, half, 0)
-
     rho[...] = jnp.zeros_like(rho)
 
-    def densities(i, _):
+    def densities(i):
         b, a = i // 4, i % 4
+        factors = jnp.concatenate([T[0, a].reshape(256, 512), T[1, a].reshape(256, 512)], axis=0)
         for sl in chunks():
-            bb = B[i, sl, :]
+            cc = dot(factors, B[i, sl, :], 1, 1)
             phi = phiR[b, a, :, sl].astype(F32)
             for k in range(2):
-                cc = dot(T[k, a].reshape(256, 512), bb, 1, 1)
-                rho[b, k : k + 1, sl] += jnp.sum(cc * phi, axis=0, keepdims=True)
+                part = cc[k * 256 : (k + 1) * 256] * phi
+                rho[b, k : k + 1, sl] += jnp.sum(part, axis=0, keepdims=True)
+
+    def both(i, _):
+        densities(i - 4)
+        half(i, 0)
         return 0
 
-    lax.fori_loop(0, 8, densities, 0)
+    def last(i, _):
+        densities(i)
+        return 0
+
+    lax.fori_loop(0, 4, half, 0)
+    for g in gt:
+        g.take(g.forward)
+        g.take(2)
+    lax.fori_loop(4, 8, both, 0)
+    lax.fori_loop(4, 8, last, 0)
     for b in range(2):
         f = wts[b : b + 1, :] * (-(4.0 / 9.0) * EXCHANGE_COEF * jnp.exp(-(2.0 / 3.0) * jnp.log(den[b : b + 1, :])))
         for k in range(2):
@@ -325,19 +333,24 @@
         ids[k]["h0"] = net.send(chunk(k, c, lows), H.at[k, 0], net.chip(d, 1))
         ids[k]["h1"] = net.send(chunk(k, c, highs), H.at[k, 1], net.chip(d, -1))
 
-    def neighbours(k):
+    def own_halves(k):
         d = dims[k]
-        for n, (s, hs) in enumerate(((1, lows), (-1, highs))):
-            c = net.at(d, s)
+        for n, (s, hs, part) in enumerate(((1, highs, 1), (-1, lows, 0))):
+            ids[k][f"o{n}"] = net.send(chunk(k, net.at(d, s), hs), A.at[k, n, pl.ds(2 * part, 2)], net.chip(d, s))
+
+    def summed_halves(k):
+        d = dims[k]
+        for n, (s, hs, part) in enumerate(((1, lows, 0), (-1, highs, 1))):
             net.arrived(ids[k][f"h{n}"], H.at[k, n])
-            part = chunk(k, c, hs)
-            part[...] = (part[...].astype(F32) + H[k, n].astype(F32)).astype(BF)
-            ids[k][f"a{n}"] = net.send(chunk(k, c), A.at[k, n], net.chip(d, s))
+            piece = chunk(k, net.at(d, s), hs)
+            piece[...] = (piece[...].astype(F32) + H[k, n].astype(F32)).astype(BF)
+            ids[k][f"a{n}"] = net.send(piece, A.at[k, n, pl.ds(2 * part, 2)], net.chip(d, s))
 
     def second(k):
         d, e = dims[k], dims[1 - k]
-        for n in range(2):
-            net.arrived(ids[k][f"a{n}"], A.at[k, n])
+        for n, part in enumerate((0, 1)):
+            net.arrived(ids[k][f"o{n}"], A.at[k, n, pl.ds(2 - 2 * part, 2)])
+            net.arrived(ids[k][f"a{n}"], A.at[k, n, pl.ds(2 * part, 2)])
         total = chunk(k, net.pos[d])[...].astype(F32) + A[k, 0].astype(F32) + A[k, 1].astype(F32)
         S[k] = total.astype(BF)
         for n, s in enumerate((2, 1, -1)):
@@ -356,12 +369,14 @@
 
     lax.fori_loop(0, 4, tiles_1, 0)
     opposite(1)
+    own_halves(1)
     tile(0, net.at("x", 2))
     opposite(0)
     tile(0, net.at("x", 1))
     tile(0, net.at("x", -1))
-    neighbours(1)
-    neighbours(0)
+    own_halves(0)
+    summed_halves(1)
+    summed_halves(0)
     tile(0, net.pos["x"])
     second(1)
     second(0)

time: 84.3 us -> 81.9 us (0.972)
  Pallas kernels: 82.4 us -> 80 us
    pallas_call x1, Pallas kernels: 82.4 us -> 80 us  [per_device(): pl.pallas_call(fused, out_shape=jax.ShapeDtypeStruct((64, 2, 512), F32),...]
where the time goes in v3:
time: 81.9 us; the launch traced here: 81.7 us
  Pallas kernels  80 us (98%)
  local copies, waits for them, and re-layouts  1.67 us (2%)
    pallas_call x1, Pallas kernels, per_device(): pl.pallas_call(fused, out_shape=jax.ShapeDtypeStruct((64, 2, 512), F32),...  80 us
    unnamed x1, local copies, waits for them, and re-layouts  1.67 us

profile of v3, /device:TPU:1, one launch (start us, length us, event | category | flops | bytes accessed | tf_op | source)
XLA Modules:
  0.0 81.7 jit_solution(10741925856339651125)
XLA Ops:
  0.0 80.0 %fused.1 = f32[64,2,512]{2,1,0:T(2,128)} custom-call(bf16[4,16,512]{2,1,0:T(8,128)(2,1)} %bitcast.7, bf16[2,64,512]{2,1,0:T(8,128)(2,1)} %tri.1, f32[3,64]{1,0:T(4,128)} %cen.1, f32[3,64]{1,0:T(4,128)} %wav.1, f32[1,64]{1,0:T(1,128)} %bitcast.10, f32[1,64]{1,0:T(1,128)} %bitcast.11, f32[3,2,1024]{2,1,0:T(2,128)} %bitcast.8, f32[2,1024]{1,0:T(2,128)} %den.1, ...), custom_call_target="tpu_custom_call" | custom-call | tf_op jit(solution)/shard_map/fused/pallas_call | solution.py:393
  80.0 1.7 %copy.13 = f32[64,2,512]{2,1,0:T(2,128)} copy(f32[64,2,512]{2,1,0:T(2,128)} %fused.1) | data formatting | bytes 524288

commit v4 on v3

--- a/solution.py
+++ b/solution.py
@@ -300,12 +300,20 @@
         densities(i)
         return 0
 
-    lax.fori_loop(0, 4, half, 0)
+    def in_twos(step, lo, hi):
+        def body(i, _):
+            step(2 * i, 0)
+            step(2 * i + 1, 0)
+            return 0
+
+        lax.fori_loop(lo // 2, hi // 2, body, 0)
+
+    in_twos(half, 0, 4)
     for g in gt:
         g.take(g.forward)
         g.take(2)
-    lax.fori_loop(4, 8, both, 0)
-    lax.fori_loop(4, 8, last, 0)
+    in_twos(both, 4, 8)
+    in_twos(last, 4, 8)
     for b in range(2):
         f = wts[b : b + 1, :] * (-(4.0 / 9.0) * EXCHANGE_COEF * jnp.exp(-(2.0 / 3.0) * jnp.log(den[b : b + 1, :])))
         for k in range(2):
@@ -367,7 +375,7 @@
         tile(1, a)
         return 0
 
-    lax.fori_loop(0, 4, tiles_1, 0)
+    in_twos(tiles_1, 0, 4)
     opposite(1)
     own_halves(1)
     tile(0, net.at("x", 2))

time: 81.9 us -> 80.4 us (0.982)
  Pallas kernels: 80 us -> 78.6 us
    pallas_call x1, Pallas kernels: 80 us -> 78.6 us  [per_device(): pl.pallas_call(fused, out_shape=jax.ShapeDtypeStruct((64, 2, 512), F32),...]
where the time goes in v4:
time: 80.4 us; the launch traced here: 80.2 us
  Pallas kernels  78.6 us (98%)
  local copies, waits for them, and re-layouts  1.67 us (2%)
    pallas_call x1, Pallas kernels, per_device(): pl.pallas_call(fused, out_shape=jax.ShapeDtypeStruct((64, 2, 512), F32),...  78.6 us
    unnamed x1, local copies, waits for them, and re-layouts  1.67 us

profile of v4, /device:TPU:1, one launch (start us, length us, event | category | flops | bytes accessed | tf_op | source)
XLA Modules:
  0.0 80.2 jit_solution(7828548186639049786)
XLA Ops:
  0.0 78.6 %fused.1 = f32[64,2,512]{2,1,0:T(2,128)} custom-call(bf16[4,16,512]{2,1,0:T(8,128)(2,1)} %bitcast.7, bf16[2,64,512]{2,1,0:T(8,128)(2,1)} %tri.1, f32[3,64]{1,0:T(4,128)} %cen.1, f32[3,64]{1,0:T(4,128)} %wav.1, f32[1,64]{1,0:T(1,128)} %bitcast.10, f32[1,64]{1,0:T(1,128)} %bitcast.11, f32[3,2,1024]{2,1,0:T(2,128)} %bitcast.8, f32[2,1024]{1,0:T(2,128)} %den.1, ...), custom_call_target="tpu_custom_call" | custom-call | tf_op jit(solution)/shard_map/fused/pallas_call | solution.py:401
  78.6 1.7 %copy.13 = f32[64,2,512]{2,1,0:T(2,128)} copy(f32[64,2,512]{2,1,0:T(2,128)} %fused.1) | data formatting | bytes 524288

commit v5 on v3

--- a/solution.py
+++ b/solution.py
@@ -300,12 +300,20 @@
         densities(i)
         return 0
 
-    lax.fori_loop(0, 4, half, 0)
+    def in_fours(step, lo):
+        def body(i, _):
+            for j in range(4):
+                step(4 * i + j, 0)
+            return 0
+
+        lax.fori_loop(lo // 4, lo // 4 + 1, body, 0)
+
+    in_fours(half, 0)
     for g in gt:
         g.take(g.forward)
         g.take(2)
-    lax.fori_loop(4, 8, both, 0)
-    lax.fori_loop(4, 8, last, 0)
+    in_fours(both, 4)
+    in_fours(last, 4)
     for b in range(2):
         f = wts[b : b + 1, :] * (-(4.0 / 9.0) * EXCHANGE_COEF * jnp.exp(-(2.0 / 3.0) * jnp.log(den[b : b + 1, :])))
         for k in range(2):
@@ -367,7 +375,7 @@
         tile(1, a)
         return 0
 
-    lax.fori_loop(0, 4, tiles_1, 0)
+    in_fours(tiles_1, 0)
     opposite(1)
     own_halves(1)
     tile(0, net.at("x", 2))

time: 81.9 us -> 79.4 us (0.969)
  Pallas kernels: 80 us -> 77.5 us
    pallas_call x1, Pallas kernels: 80 us -> 77.5 us  [per_device(): pl.pallas_call(fused, out_shape=jax.ShapeDtypeStruct((64, 2, 512), F32),...]
where the time goes in v5:
time: 79.4 us; the launch traced here: 79.2 us
  Pallas kernels  77.5 us (98%)
  local copies, waits for them, and re-layouts  1.67 us (2%)
    pallas_call x1, Pallas kernels, per_device(): pl.pallas_call(fused, out_shape=jax.ShapeDtypeStruct((64, 2, 512), F32),...  77.5 us
    unnamed x1, local copies, waits for them, and re-layouts  1.67 us

profile of v5, /device:TPU:1, one launch (start us, length us, event | category | flops | bytes accessed | tf_op | source)
XLA Modules:
  0.0 79.2 jit_solution(10404791289927000727)
XLA Ops:
  0.0 77.5 %fused.1 = f32[64,2,512]{2,1,0:T(2,128)} custom-call(bf16[4,16,512]{2,1,0:T(8,128)(2,1)} %bitcast.7, bf16[2,64,512]{2,1,0:T(8,128)(2,1)} %tri.1, f32[3,64]{1,0:T(4,128)} %cen.1, f32[3,64]{1,0:T(4,128)} %wav.1, f32[1,64]{1,0:T(1,128)} %bitcast.10, f32[1,64]{1,0:T(1,128)} %bitcast.11, f32[3,2,1024]{2,1,0:T(2,128)} %bitcast.8, f32[2,1024]{1,0:T(2,128)} %den.1, ...), custom_call_target="tpu_custom_call" | custom-call | tf_op jit(solution)/shard_map/fused/pallas_call | solution.py:401
  77.6 1.7 %copy.13 = f32[64,2,512]{2,1,0:T(2,128)} copy(f32[64,2,512]{2,1,0:T(2,128)} %fused.1) | data formatting | bytes 524288
